TPU v7x, 32 devices: a whole 2x2x4 slice. The times are simulated.
32 devices in a mesh: gx: 4 (over x, core), gy: 4 (over z), gz: 2 (over y).
Axes of the slice: x: 2, y: 2, z: 4, core: 2. Of those that a mesh axis runs over, the one named last changes fastest.
Arguments:
- layer_input: bfloat16 [1024, 4096], P('gz', ('gx', 'gy')), may hold values from -6 to 6
- modality: int32 [1024], P('gz'), may hold values 0 or 1
- image_spans: int32 [2, 8], replicated, may hold values from 0 to 1024, as said below
- norm_gain: float32 [2, 4096], P(None, ('gx', 'gy')), may hold values from 0.1 to 1.9
- w_qkv: bfloat16 [3, 4096, 2048], P(None, 'gz', ('gx', 'gy')), as said below
- w_out: bfloat16 [2048, 4096], P(('gx', 'gy'), 'gz'), may hold values from -0.125 to 0.125
- grad_out: bfloat16 [1024, 4096], P('gz', ('gx', 'gy')), may hold values from -6 to 6
Outputs:
- attn_out: bfloat16 [1024, 4096], P('gz', ('gx', 'gy'))
- grad_in: bfloat16 [1024, 4096], P('gz', ('gx', 'gy'))
- grad_qkv: float32 [3, 4096, 2048], P(None, 'gz', ('gx', 'gy'))
- grad_wout: float32 [2048, 4096], P(('gx', 'gy'), 'gz')
- grad_gain: float32 [2, 4096], P(None, ('gx', 'gy'))
Inputs may be any that keep to these rules, and one draw needn't show every extreme that they name: `image_spans`: row 0 holds the first position of each of 8 image spans, in increasing order, and row 1 one past its last; spans are disjoint and none is empty. `w_qkv`: entries are at most 20 * 4096 ** -0.5 in magnitude.
All inputs are finite; a program needn't handle non-finite values. No bound on the sum of `modality` on one device may be relied on, other than what follows from the above.
Results may differ from a plain program's by a relative error of at most 0.035.
The roundings to bfloat16 on the way count: a program that leaves them out, or rounds other values in their place, can miss the bound.
Values may be sent and summed in bfloat16 or wider, within the bound.
A program may use at most 128 MiB of HBM per device.

v0:
```python
import math
import jax
import jax.numpy as jnp
from jax import lax
from jax.sharding import PartitionSpec as P

epsilon = 1e-05
masked_low = -1e30


def span_index(positions, image_spans):
    inside = (positions[:, None] >= image_spans[0][None, :]) & (
        positions[:, None] < image_spans[1][None, :]
    )
    labels = jnp.arange(1, image_spans.shape[1] + 1, dtype=jnp.int32)
    return jnp.sum(jnp.where(inside, labels[None, :], 0), axis=1) - 1


def visible(query_pos, query_span, key_pos, key_span):
    causal = key_pos[None, :] <= query_pos[:, None]
    same_image = (query_span[:, None] == key_span[None, :]) & (query_span[:, None] >= 0)
    return causal | same_image


def per_device(layer_input, modality, image_spans, norm_gain, w_qkv, w_out, grad_out):
    tok_rows, local_width = layer_input.shape
    full_width = local_width * lax.axis_size(("gx", "gy"))
    head_dim = w_qkv.shape[2]
    inputs_f = layer_input.astype(jnp.float32)
    squares = lax.psum(jnp.sum(inputs_f * inputs_f, axis=1), ("gx", "gy"))
    inv_rms = lax.rsqrt(squares / full_width + epsilon)
    row_gain = jnp.where(modality[:, None] == 1, norm_gain[1][None, :], norm_gain[0][None, :])
    scaled = inputs_f * inv_rms[:, None]
    normed = (scaled * row_gain).astype(jnp.bfloat16)
    w_full = lax.all_gather(w_qkv, "gz", axis=1, tiled=True)
    wo_full = lax.all_gather(w_out, "gz", axis=1, tiled=True)
    rows_block = w_full
    projected = jnp.einsum(
        "tc,mch->mth",
        lax.all_gather(normed, ("gx", "gy"), axis=1, tiled=True),
        rows_block,
        preferred_element_type=jnp.float32,
    )
    projected = projected.astype(jnp.bfloat16)
    queries = projected[0]
    keys_values = lax.all_gather(
        jnp.concatenate([projected[1], projected[2]], axis=1), "gz", axis=0, tiled=True
    )
    key_total = keys_values.shape[0]
    query_pos = lax.axis_index("gz") * tok_rows + jnp.arange(tok_rows, dtype=jnp.int32)
    query_span = span_index(query_pos, image_spans)
    key_block = 512
    block_count = key_total // key_block
    score_scale = 1.0 / math.sqrt(head_dim)
    block_ids = jnp.arange(block_count, dtype=jnp.int32)

    def block_scores(block_idx):
        first_key = block_idx * key_block
        kv_block = lax.dynamic_slice_in_dim(keys_values, first_key, key_block, 0)
        key_pos = first_key + jnp.arange(key_block, dtype=jnp.int32)
        allowed = visible(query_pos, query_span, key_pos, span_index(key_pos, image_spans))
        scores = (
            lax.dot_general(
                queries,
                kv_block[:, :head_dim],
                (((1,), (1,)), ((), ())),
                preferred_element_type=jnp.float32,
            )
            * score_scale
        )
        return (kv_block, allowed, scores)

    def gather_stats(state, block_idx):
        maxima, summed = state
        kv_block, allowed, scores = block_scores(block_idx)
        new_maxima = jnp.maximum(maxima, jnp.max(jnp.where(allowed, scores, masked_low), axis=1))
        fresh = jnp.sum(jnp.where(allowed, jnp.exp(scores - new_maxima[:, None]), 0.0), axis=1)
        return ((new_maxima, summed * jnp.exp(maxima - new_maxima) + fresh), None)

    start_state = (
        jnp.full((tok_rows,), masked_low, jnp.float32),
        jnp.zeros((tok_rows,), jnp.float32),
    )
    (maxima, summed), unused = lax.scan(gather_stats, start_state, block_ids)
    lse = maxima + jnp.log(summed)

    def block_probs(block_idx):
        kv_block, allowed, scores = block_scores(block_idx)
        return (kv_block, jnp.where(allowed, jnp.exp(scores - lse[:, None]), 0.0))

    def attend(accum, block_idx):
        kv_block, attn_p = block_probs(block_idx)
        return (
            accum
            + jnp.dot(
                attn_p.astype(jnp.bfloat16),
                kv_block[:, head_dim:],
                preferred_element_type=jnp.float32,
            ),
            None,
        )

    attended_f, unused = lax.scan(attend, jnp.zeros((tok_rows, head_dim), jnp.float32), block_ids)
    attended = attended_f.astype(jnp.bfloat16)
    all_heads = lax.all_gather(attended, ("gx", "gy"), axis=1, tiled=True)
    out_rows = lax.all_to_all(wo_full, ("gx", "gy"), split_axis=1, concat_axis=0, tiled=True)
    head_total = out_rows.shape[0] // head_dim
    per_head = jnp.einsum(
        "thd,hdc->htc",
        all_heads.reshape(tok_rows, head_total, head_dim),
        out_rows.reshape(head_total, head_dim, local_width),
        preferred_element_type=jnp.float32,
    )
    per_head = lax.optimization_barrier(per_head.astype(jnp.bfloat16)).astype(jnp.float32)
    attn_out = jnp.sum(per_head, axis=0).astype(jnp.bfloat16)
    segment = lax.all_gather(grad_out, ("gx", "gy"), axis=1, tiled=True)
    d_accum = lax.dot_general(
        segment, wo_full, (((1,), (1,)), ((), ())), preferred_element_type=jnp.float32
    )
    partial_value = lax.dot_general(
        attended, segment, (((0,), (0,)), ((), ())), preferred_element_type=jnp.float32
    )
    d_attended = d_accum.astype(jnp.bfloat16)
    row_dots = jnp.sum(d_attended.astype(jnp.float32) * attended.astype(jnp.float32), axis=1)

    def backward_block(d_query, block_idx):
        kv_block, attn_p = block_probs(block_idx)
        d_probs = lax.dot_general(
            d_attended,
            kv_block[:, head_dim:],
            (((1,), (1,)), ((), ())),
            preferred_element_type=jnp.float32,
        )
        d_scores = (attn_p * (d_probs - row_dots[:, None]) * score_scale).astype(jnp.bfloat16)
        d_query = d_query + jnp.dot(
            d_scores, kv_block[:, :head_dim], preferred_element_type=jnp.float32
        )
        d_keys = lax.dot_general(
            d_scores, queries, (((0,), (0,)), ((), ())), preferred_element_type=jnp.float32
        )
        d_values = lax.dot_general(
            attn_p.astype(jnp.bfloat16),
            d_attended,
            (((0,), (0,)), ((), ())),
            preferred_element_type=jnp.float32,
        )
        return (d_query, jnp.concatenate([d_keys, d_values], axis=1))

    d_query_f, kv_parts = lax.scan(
        backward_block, jnp.zeros((tok_rows, head_dim), jnp.float32), block_ids
    )
    kv_grad = lax.psum_scatter(
        kv_parts.reshape(key_total, 2 * head_dim).astype(jnp.bfloat16),
        "gz",
        scatter_dimension=0,
        tiled=True,
    ).astype(jnp.float32)
    grads = jnp.stack(
        [
            d_query_f.astype(jnp.bfloat16),
            kv_grad[:, :head_dim].astype(jnp.bfloat16),
            kv_grad[:, head_dim:].astype(jnp.bfloat16),
        ]
    )
    w_grad = jnp.einsum(
        "tc,mth->mch",
        lax.all_gather(normed, ("gx", "gy"), axis=1, tiled=True),
        grads,
        preferred_element_type=jnp.float32,
    )
    grad_qkv, grad_wout = (
        lax.psum_scatter(w_grad.astype(jnp.bfloat16), "gz", scatter_dimension=1, tiled=True).astype(
            jnp.float32
        ),
        lax.psum_scatter(
            partial_value.astype(jnp.bfloat16), "gz", scatter_dimension=1, tiled=True
        ).astype(jnp.float32),
    )
    rows_block = w_full
    grad_normed = (
        lax.psum_scatter(
            jnp.einsum("mch,mth->ct", rows_block, grads, preferred_element_type=jnp.float32).astype(
                jnp.bfloat16
            ),
            ("gx", "gy"),
            scatter_dimension=0,
            tiled=True,
        )
        .astype(jnp.float32)
        .T
    )
    upstream = grad_normed * row_gain
    norm_dots = lax.psum(jnp.sum(upstream * scaled, axis=1), ("gx", "gy"))
    grad_in = (inv_rms[:, None] * (upstream - scaled * (norm_dots / full_width)[:, None])).astype(
        jnp.bfloat16
    )
    onehot = (modality[:, None] == jnp.arange(2, dtype=jnp.int32)[None, :]).astype(jnp.float32)
    local_gain = jnp.dot(onehot.T, grad_normed * scaled, precision=lax.Precision.HIGHEST)
    grad_gain = lax.psum(local_gain, "gz")
    return (attn_out, grad_in, grad_qkv, grad_wout, grad_gain)


def solution(mesh):
    in_specs = (
        P("gz", ("gx", "gy")),
        P("gz"),
        P(),
        P(None, ("gx", "gy")),
        P(None, "gz", ("gx", "gy")),
        P(("gx", "gy"), "gz"),
        P("gz", ("gx", "gy")),
    )
    out_specs = (
        P("gz", ("gx", "gy")),
        P("gz", ("gx", "gy")),
        P(None, "gz", ("gx", "gy")),
        P(("gx", "gy"), "gz"),
        P(None, ("gx", "gy")),
    )
    return jax.shard_map(
        per_device, mesh=mesh, in_specs=in_specs, out_specs=out_specs, check_vma=False
    )
```

profile of v0, /device:TPU:0, one launch (start us, length us, event | category | flops | bytes accessed | tf_op | source)
XLA Modules:
  0.0 420.7 jit_solution(4267195177550142330)
XLA Ops:
  7.3 2.7 copy.44
  10.2 35.2 %psum.21 = f32[512]{0:T(512)S(1)} all-reduce(f32[512]{0:T(512)S(1)} %fusion.65), channel_id=1, replica_groups=mesh['gx'=4,'gy'=4,'gz'=2] {'gx','gy'}, use_global_device_ids=true, to_apply=%region_1.0 | all-reduce | flops 512 | bytes 4096 | tf_op jit(solution)/shard_map/psum | solution.py:30
  48.3 9.5 %all-gather.8.cloned.1.call-done = bf16[3,4096,128]{1,2,0:T(8,128)(2,1)} async-done(((bf16[3,2048,128]{1,2,0:T(8,128)(2,1)}), bf16[3,4096,128]{1,2,0:T(8,128)(2,1)}) %all-gather.8.cloned.1.call-update) | async-done | bytes 3145744 | tf_op jit(solution)/shard_map/all_gather | solution.py:35
  57.8 55.2 %all-gather.6.cloned.1.call-done = bf16[512,4096]{1,0:T(8,128)(2,1)} async-done(((bf16[512,256]{1,0:T(8,128)(2,1)}), bf16[512,4096]{1,0:T(8,128)(2,1)}) %all-gather.6.cloned.1.call-update) | async-done | bytes 4194320 | tf_op jit(solution)/shard_map/all_gather | solution.py:40
  113.0 5.0 %fusion.75 = f32[512,384]{0,1:S(1)} fusion(bf16[512,4096]{1,0:T(8,128)(2,1)} %all-gather.6.cloned.1.call-done, bf16[4096,384]{0,1:T(8,128)(2,1)} %bitcast.156), kind=kOutput, calls=%fused_computation.134 | convolution fusion | flops 1610612736 | bytes 8126464
  118.1 13.9 %all_gather.21 = bf16[1024,256]{0,1:T(8,128)(2,1)S(1)} all-gather(bf16[512,256]{0,1:T(8,128)(2,1)S(1)} %pad_maximum_fusion.1), channel_id=1, replica_groups=mesh['gx'=4,'gy'=4,'gz'=2] {'gz'}, dimensions={0}, use_global_device_ids=true | all-gather | bytes 786432 | tf_op jit(solution)/shard_map/all_gather | solution.py:46
  132.4 4.8 %while.43 = (s32[]{:T(128)}, f32[512]{0:T(512)S(1)}, f32[512]{0:T(512)S(1)}, s32[2]{0:T(128)S(1)}, s32[512]{0:T(512)S(1)}, /*index=5*/s32[2,8]{1,0:T(2,128)S(1)}...) while((s32[]{:T(128)}, f32[512]{0:T(512)S(1)}, ...), condition=%wide.region_7.8_spmd.clone, body=%wide.region_3.7_spmd.clone.sunk | while | flops 70803472 | bytes 2418638 | solution.py:84
  137.7 5.9 %while.44 = (s32[]{:T(128)}, f32[512,128]{1,0:T(8,128)S(1)}, s32[2]{0:T(128)S(1)}, s32[512]{0:T(512)S(1)}, s32[2,8]{1,0:T(2,128)S(1)}, /*index=5*/bf16[1024,256]...) while((s32[]{:T(128)}, f32[512,128]{1,0:T(8,128)S(1)}, ...), condition=%wide.region_10.11_spmd.clone, body=%wide.region_8.10_spmd.clone.sunk | while | flops 136467984 | bytes 945628 | solution.py:103
  139.1 1.5 fusion.118
  142.1 1.5 fusion.118
  143.8 47.6 %all-gather.14.cloned.1.call-done = bf16[512,4096]{1,0:T(8,128)(2,1)} async-done(((bf16[512,256]{1,0:T(8,128)(2,1)}), bf16[512,4096]{1,0:T(8,128)(2,1)}) %all-gather.14.cloned.1.call-update) | async-done | bytes 4194320 | tf_op jit(solution)/shard_map/all_gather | solution.py:116
  191.3 4.0 multiply_reduce_fusion
  196.0 9.3 %while.45 = (s32[]{:T(128)}, f32[512,128]{1,0:T(8,128)S(1)}, bf16[2,512,256]{1,2,0:T(8,128)(2,1)S(1)}, s32[2]{0:T(128)}, s32[512]{0:T(512)S(1)}, /*index=5*/s32[...) while((s32[]{:T(128)}, f32[512,128]{1,0:T(8,128)S(1)}, ...), condition=%wide.region_15.16_spmd.clone, body=%wide.region_13.15_spmd.clone.sunk | while | flops 339367424 | bytes 6974985 | solution.py:149
  206.4 3.9 convolution_convert_fusion.1
  211.1 8.2 %reduce-scatter.5.cloned.1.call-done = bf16[512,256]{1,0:T(8,128)(2,1)} async-done(((bf16[1024,256]{1,0:T(8,128)(2,1)}), bf16[512,256]{1,0:T(8,128)(2,1)}) %reduce-scatter.5.cloned.1.call-update) | async-done | bytes 262160 | tf_op jit(solution)/shard_map/reduce_scatter | solution.py:152
  220.2 5.8 %fusion.52 = bf16[4096,512]{0,1:T(8,128)(2,1)} fusion(bf16[3,4096,128]{1,2,0:T(8,128)(2,1)} %all-gather.8.cloned.1.call-done, bf16[1,512,128]{2,1,0:T(8,128)(2,1)S(1)} %get-tuple-element.678, bf16[1,512,128]{2,1,0:T(8,128)(2,1)S(1)} %get-tuple-element.677, bf16[1,512,128]{2,1,0:T(8,128)(2,1)S(1)} %convert_bitcast_fusion.1), kind=kOutput, calls=%fused_computation.84 | convolution fusion | flops 1613103104 | bytes 7733248 | tf_op jit(solution)/shard_map/mch,mth->ct/dot_general | solution.py:182
  226.3 6.1 %fusion.53 = bf16[3,4096,128]{1,2,0:T(8,128)(2,1)} fusion(bf16[512,4096]{1,0:T(8,128)(2,1)} %all-gather.6.cloned.1.call-done, bf16[1,512,128]{2,1,0:T(8,128)(2,1)S(1)} %get-tuple-element.678, bf16[1,512,128]{2,1,0:T(8,128)(2,1)S(1)} %get-tuple-element.677, bf16[1,512,128]{2,1,0:T(8,128)(2,1)S(1)} %convert_bitcast_fusion.1), kind=kOutput, calls=%fused_computation.85 | convolution fusion | flops 1612578816 | bytes 7733248 | tf_op jit(solution)/shard_map/tc,mth->mch/dot_general | solution.py:165
  232.4 1.3 copy.51
  233.8 5.5 %all-to-all-start = ((bf16[128,16,256]{2,0,1:T(8,128)(2,1)}), bf16[128,16,256]{2,0,1:T(8,128)(2,1)S(1)}, u32[]{:S(2)}, u32[]{:S(2)}) async-start(bf16[128,16,256]{2,0,1:T(8,128)(2,1)} %copy.51), calls=%async_computation | async-start | bytes 2097152 | tf_op jit(solution)/shard_map/all_to_all | solution.py:106
  239.3 3.1 reduce-scatter.11.cloned.1.call-done
  242.4 2.1 convert_element_type.104
  244.5 25.8 %all-to-all-done = bf16[128,16,256]{2,0,1:T(8,128)(2,1)S(1)} async-done(((bf16[128,16,256]{2,0,1:T(8,128)(2,1)}), bf16[128,16,256]{2,0,1:T(8,128)(2,1)S(1)}, u32[]{:S(2)}, u32[]{:S(2)}) %all-to-all-start) | async-done | bytes 1048608 | tf_op jit(solution)/shard_map/all_to_all | solution.py:106
  270.3 19.1 %all-gather.10.cloned.1.call-done = bf16[512,2048]{0,1:T(8,128)(2,1)} async-done(((bf16[512,128]{0,1:T(8,128)(2,1)}), bf16[512,2048]{0,1:T(8,128)(2,1)}) %all-gather.10.cloned.1.call-update) | async-done | bytes 2097168 | tf_op jit(solution)/shard_map/all_gather | solution.py:105
  289.4 4.8 %convolution_convert_fusion.2 = bf16[16,512,256]{2,1,0:T(8,128)(2,1)} fusion(bf16[512,16,128]{0,2,1:T(8,128)(2,1)} %bitcast.147, bf16[128,16,256]{2,0,1:T(8,128)(2,1)S(1)} %all-to-all-done), kind=kOutput, calls=%fused_computation.88 | convolution fusion | flops 538968064 | bytes 7340032 | tf_op jit(solution)/shard_map/thd,hdc->htc/dot_general | solution.py:108
  294.2 3.5 reduce_sum.98
  297.8 67.0 %reduce-scatter.7.cloned.1.call-done = bf16[256,512]{0,1:T(8,128)(2,1)} async-done(((bf16[4096,512]{0,1:T(8,128)(2,1)}), bf16[256,512]{0,1:T(8,128)(2,1)}) %reduce-scatter.7.cloned.1.call-update) | async-done | bytes 262160 | tf_op jit(solution)/shard_map/reduce_scatter | solution.py:181
  364.8 1.3 fusion.59
  366.1 30.5 %psum.22 = f32[512]{0:T(512)S(1)} all-reduce(f32[512]{0:T(512)S(1)} %fusion.59), channel_id=1, replica_groups=mesh['gx'=4,'gy'=4,'gz'=2] {'gx','gy'}, use_global_device_ids=true, to_apply=%region_19.20 | all-reduce | flops 512 | bytes 4096 | tf_op jit(solution)/shard_map/psum | solution.py:193
  396.6 1.5 fusion.63
  398.1 5.7 %psum.23 = f32[2,256]{1,0:T(2,128)} all-reduce(f32[2,256]{1,0:T(2,128)S(1)} %fusion.63), channel_id=1, replica_groups=mesh['gx'=4,'gy'=4,'gz'=2] {'gz'}, use_global_device_ids=true, to_apply=%region_22.23 | all-reduce | flops 512 | bytes 4096 | tf_op jit(solution)/shard_map/psum | solution.py:199
  403.8 6.4 %reduce-scatter.9.cloned.1.call-done = bf16[3,2048,128]{1,2,0:T(8,128)(2,1)} async-done(((bf16[3,4096,128]{1,2,0:T(8,128)(2,1)}), bf16[3,2048,128]{1,2,0:T(8,128)(2,1)}) %reduce-scatter.9.cloned.1.call-update) | async-done | bytes 1572880 | tf_op jit(solution)/shard_map/reduce_scatter | solution.py:172
  410.2 3.1 copy.59
  (145 shorter events, 21.4 us)
Async XLA Ops:
  7.2 2.8 copy-start
  7.2 38.2 %copy-start.12 = (s32[512]{0:T(512)S(1)}, s32[512]{0:T(512)}, u32[]{:S(2)}) copy-start(s32[512]{0:T(512)} %param.14) | copy-start | bytes 6148
  7.2 38.2 %copy-start.14 = (f32[2,256]{1,0:T(2,128)S(1)}, f32[2,256]{1,0:T(2,128)}, u32[]{:S(2)}) copy-start(f32[2,256]{1,0:T(2,128)} %param.16) | copy-start | bytes 6148
  7.2 39.2 %copy-start.4 = (bf16[128,2048]{1,0:T(8,128)(2,1)S(1)}, bf16[128,2048]{1,0:T(8,128)(2,1)}, u32[]{:S(2)}) copy-start(bf16[128,2048]{1,0:T(8,128)(2,1)} %param.18) | copy-start | bytes 1572868
  7.2 41.0 %copy-start.5 = (s32[2,8]{1,0:T(2,128)S(1)}, s32[2,8]{1,0:T(2,128)}, u32[]{:S(2)}) copy-start(s32[2,8]{1,0:T(2,128)} %param.15) | copy-start | bytes 196
  7.2 50.6 %all-gather.8.cloned.1.call-start = ((), (), s32[]{:S(2)}) async-start(), calls=%async_computation.6 | async-start | bytes 4718592 | tf_op jit(solution)/shard_map/all_gather | solution.py:35
  10.0 103.0 %all-gather.6.cloned.1.call-start = ((), (), s32[]{:S(2)}) async-start(), calls=%async_computation.5 | async-start | bytes 4456448 | tf_op jit(solution)/shard_map/all_gather | solution.py:40
  45.4 2.8 copy-start.10
  45.4 2.7 copy-start.8
  45.4 72.6 %copy-start.6 = (f32[1,256]{1,0:T(1,128)}, f32[1,256]{1,0:T(1,128)S(1)}, u32[]{:S(2)}) copy-start(f32[1,256]{1,0:T(1,128)S(1)} %get-tuple-element.679) | copy-start | bytes 3076
  46.3 97.4 %all-gather.12.cloned.1.call-start = ((), (), s32[]{:S(2)}) async-start(), calls=%async_computation.8 | async-start | bytes 1572864 | tf_op jit(solution)/shard_map/all_gather | solution.py:36
  47.4 143.9 %all-gather.14.cloned.1.call-start = ((), (), s32[]{:S(2)}) async-start(), calls=%async_computation.9 | async-start | bytes 4456448 | tf_op jit(solution)/shard_map/all_gather | solution.py:116
  48.0 171.2 %reduce-scatter.5.cloned.1.call-start = ((), (), s32[]{:S(2)}) async-start(), calls=%async_computation.10 | async-start | bytes 786432 | tf_op jit(solution)/shard_map/reduce_scatter | solution.py:152
  143.7 62.6 %copy-start.2 = (bf16[512,128]{0,1:T(8,128)(2,1)}, bf16[512,128]{0,1:T(8,128)(2,1)S(1)}, u32[]{:S(2)}) copy-start(bf16[512,128]{0,1:T(8,128)(2,1)S(1)} %copy.49) | copy-start | bytes 393220
  206.3 36.1 %reduce-scatter.11.cloned.1.call-start = ((), (), s32[]{:S(2)}) async-start(), calls=%async_computation.13 | async-start | bytes 1572864 | tf_op jit(solution)/shard_map/reduce_scatter | solution.py:175
  210.3 79.1 %all-gather.10.cloned.1.call-start = ((), (), s32[]{:S(2)}) async-start(), calls=%async_computation.7 | async-start | bytes 2228224 | tf_op jit(solution)/shard_map/all_gather | solution.py:105
  211.0 153.8 %reduce-scatter.7.cloned.1.call-start = ((), (), s32[]{:S(2)}) async-start(), calls=%async_computation.11 | async-start | bytes 4456448 | tf_op jit(solution)/shard_map/reduce_scatter | solution.py:181
  226.1 6.4 %copy-start.1 = (bf16[128,4096]{0,1:T(8,128)(2,1)S(1)}, bf16[128,4096]{0,1:T(8,128)(2,1)}, u32[]{:S(2)}) copy-start(bf16[128,4096]{0,1:T(8,128)(2,1)} %all-gather.12.cloned.1.call-done) | copy-start | bytes 3145732
  226.1 184.1 %reduce-scatter.9.cloned.1.call-start = ((), (), s32[]{:S(2)}) async-start(), calls=%async_computation.12 | async-start | bytes 4718592 | tf_op jit(solution)/shard_map/reduce_scatter | solution.py:172
  233.8 36.5 %all-to-all-start = ((bf16[128,16,256]{2,0,1:T(8,128)(2,1)}), bf16[128,16,256]{2,0,1:T(8,128)(2,1)S(1)}, u32[]{:S(2)}, u32[]{:S(2)}) async-start(bf16[128,16,256]{2,0,1:T(8,128)(2,1)} %copy.51), calls=%async_computation | async-start | bytes 2097152 | tf_op jit(solution)/shard_map/all_to_all | solution.py:106
  289.4 75.4 %copy-start.7 = (f32[1,256]{1,0:T(1,128)S(1)}, f32[1,256]{1,0:T(1,128)}, u32[]{:S(2)}) copy-start(f32[1,256]{1,0:T(1,128)} %copy-done.6) | copy-start | bytes 3076
  289.4 75.4 %copy-start.9 = (f32[1,256]{1,0:T(1,128)S(1)}, f32[1,256]{1,0:T(1,128)}, u32[]{:S(2)}) copy-start(f32[1,256]{1,0:T(1,128)} %copy-done.8) | copy-start | bytes 3076
  289.4 75.4 %copy-start.11 = (pred[512]{0:T(512)(128)(4,1)S(1)}, pred[512]{0:T(512)(128)(4,1)}, u32[]{:S(2)}) copy-start(pred[512]{0:T(512)(128)(4,1)} %copy-done.10) | copy-start | bytes 1540
  294.2 102.4 %copy-start.13 = (s32[512]{0:T(512)S(1)}, s32[512]{0:T(512)}, u32[]{:S(2)}) copy-start(s32[512]{0:T(512)} %param.14) | copy-start | bytes 6148
  364.8 48.5 %copy-start.3 = (bf16[256,512]{0,1:T(8,128)(2,1)S(1)}, bf16[256,512]{0,1:T(8,128)(2,1)}, u32[]{:S(2)}) copy-start(bf16[256,512]{0,1:T(8,128)(2,1)} %reduce-scatter.7.cloned.1.call-done) | copy-start | bytes 786436
Sparse Core Ops, SparseCore 0:
  10.1 47.6 all-gather.7
  60.5 52.4 all-gather.5
  115.1 23.5 all-gather.11
  140.6 50.6 all-gather.13
  206.4 12.7 reduce-scatter.4
  221.9 20.3 reduce-scatter.10
  245.1 44.2 all-gather.9
  293.3 71.4 reduce-scatter.6
  367.6 42.5 reduce-scatter.8
where the time goes:
time: 421 us
  waiting for transfers between devices  243 us (58%)
  blocking collectives  85.3 us (20%)
  matrix products  40.2 us (10%)
  local copies, waits for them, and re-layouts  16.1 us (4%)
  between operations  14.2 us (3%)
  other arithmetic  11.5 us (3%)
  starting transfers between devices  6.02 us (1%)
  loops' own time  4.31 us (1%)
    reduce_scatter x1, waiting for transfers between devices, per_device(): lax.psum_scatter(jnp.einsum('mch,mth->ct', rows_block, grads, preferred_e...  67 us
    all_gather x1, waiting for transfers between devices, per_device(): lax.all_gather(normed, ('gx', 'gy'), axis=1, tiled=True)  55.2 us
    all_gather x1, waiting for transfers between devices, per_device(): segment = lax.all_gather(grad_out, ('gx', 'gy'), axis=1, tiled=True)  47.6 us
    psum x1, blocking collectives, per_device(): squares = lax.psum(jnp.sum(inputs_f * inputs_f, axis=1), ('gx', 'gy'))  35.2 us
    psum x1, blocking collectives, per_device(): norm_dots = lax.psum(jnp.sum(upstream * scaled, axis=1), ('gx', 'gy'))  30.5 us
    all_to_all x1, waiting for transfers between devices, per_device(): lax.all_to_all(wo_full, ('gx', 'gy'), split_axis=1, concat_axis=0, tiled=...  25.8 us
    all_gather x1, waiting for transfers between devices, per_device(): all_heads = lax.all_gather(attended, ('gx', 'gy'), axis=1, tiled=True)  19.1 us
    all_gather x1, blocking collectives, per_device(): lax.all_gather(jnp.concatenate([projected[1], projected[2]], axis=1), 'gz...  13.9 us
  transfers between devices with their start and end apart: 10, of which 9 were waited for; matrix products, arithmetic and copies ran while one was open for 11% of the time, Pallas kernels for 0%

commit v1 on v0

--- a/solution.py
+++ b/solution.py
@@ -27,7 +27,7 @@
     full_width = local_width * lax.axis_size(("gx", "gy"))
     head_dim = w_qkv.shape[2]
     inputs_f = layer_input.astype(jnp.float32)
-    squares = lax.psum(jnp.sum(inputs_f * inputs_f, axis=1), ("gx", "gy"))
+    squares = jnp.sum(lax.all_gather(jnp.sum(inputs_f * inputs_f, axis=1), ("gx", "gy")), axis=0)
     inv_rms = lax.rsqrt(squares / full_width + epsilon)
     row_gain = jnp.where(modality[:, None] == 1, norm_gain[1][None, :], norm_gain[0][None, :])
     scaled = inputs_f * inv_rms[:, None]

time: 421 us -> 421 us (level)
    psum x1 -> x0, blocking collectives: 35.2 us -> none  [per_device(): squares = lax.psum(jnp.sum(inputs_f * inputs_f, axis=1), ('gx', 'gy'))]
    all_gather x0 -> x1, blocking collectives: none -> 34.1 us  [per_device(): lax.all_gather(jnp.sum(inputs_f * inputs_f, axis=1), ('gx', 'gy'))]
where the time goes in v1:
time: 421 us
  waiting for transfers between devices  244 us (58%)
  blocking collectives  84.2 us (20%)
  matrix products  40.2 us (10%)
  local copies, waits for them, and re-layouts  16.1 us (4%)
  between operations  14.2 us (3%)
  other arithmetic  11.5 us (3%)
  starting transfers between devices  6.02 us (1%)
  loops' own time  4.31 us (1%)
    reduce_scatter x1, waiting for transfers between devices, per_device(): lax.psum_scatter(jnp.einsum('mch,mth->ct', rows_block, grads, preferred_e...  67 us
    all_gather x1, waiting for transfers between devices, per_device(): lax.all_gather(normed, ('gx', 'gy'), axis=1, tiled=True)  55.2 us
    all_gather x1, waiting for transfers between devices, per_device(): segment = lax.all_gather(grad_out, ('gx', 'gy'), axis=1, tiled=True)  47.6 us
    all_gather x1, blocking collectives, per_device(): lax.all_gather(jnp.sum(inputs_f * inputs_f, axis=1), ('gx', 'gy'))  34.1 us
    psum x1, blocking collectives, per_device(): norm_dots = lax.psum(jnp.sum(upstream * scaled, axis=1), ('gx', 'gy'))  30.5 us
    all_to_all x1, waiting for transfers between devices, per_device(): lax.all_to_all(wo_full, ('gx', 'gy'), split_axis=1, concat_axis=0, tiled=...  25.8 us
    all_gather x1, waiting for transfers between devices, per_device(): all_heads = lax.all_gather(attended, ('gx', 'gy'), axis=1, tiled=True)  19.1 us
    all_gather x1, blocking collectives, per_device(): lax.all_gather(jnp.concatenate([projected[1], projected[2]], axis=1), 'gz...  13.9 us
  transfers between devices with their start and end apart: 10, of which 9 were waited for; matrix products, arithmetic and copies ran while one was open for 11% of the time, Pallas kernels for 0%

profile of v1, /device:TPU:0, one launch (start us, length us, event | category | flops | bytes accessed | tf_op | source)
XLA Modules:
  0.0 420.7 jit_solution(6988923968176401827)
XLA Ops:
  7.3 2.7 copy.61
  10.2 34.1 %all-gather.1 = f32[16,1,512]{2,1,0:T(1,128)S(1)} all-gather(f32[1,1,512]{2,1,0:T(1,128)S(1)} %bitcast.157), channel_id=2, replica_groups=mesh['gx'=4,'gy'=4,'gz'=2] {'gx','gy'}, dimensions={0}, use_global_device_ids=true | all-gather | bytes 34816 | tf_op jit(solution)/shard_map/all_gather | solution.py:30
  47.2 10.6 %all-gather.10.cloned.1.call-done = bf16[3,4096,128]{1,2,0:T(8,128)(2,1)} async-done(((bf16[3,2048,128]{1,2,0:T(8,128)(2,1)}), bf16[3,4096,128]{1,2,0:T(8,128)(2,1)}) %all-gather.10.cloned.1.call-update) | async-done | bytes 3145744 | tf_op jit(solution)/shard_map/all_gather | solution.py:35
  57.8 55.2 %all-gather.8.cloned.1.call-done = bf16[512,4096]{1,0:T(8,128)(2,1)} async-done(((bf16[512,256]{1,0:T(8,128)(2,1)}), bf16[512,4096]{1,0:T(8,128)(2,1)}) %all-gather.8.cloned.1.call-update) | async-done | bytes 4194320 | tf_op jit(solution)/shard_map/all_gather | solution.py:40
  113.0 5.0 %fusion.75 = f32[512,384]{0,1:S(1)} fusion(bf16[512,4096]{1,0:T(8,128)(2,1)} %all-gather.8.cloned.1.call-done, bf16[4096,384]{0,1:T(8,128)(2,1)} %bitcast.158), kind=kOutput, calls=%fused_computation.134 | convolution fusion | flops 1610612736 | bytes 8126464
  118.1 13.9 %all_gather.29 = bf16[1024,256]{0,1:T(8,128)(2,1)S(1)} all-gather(bf16[512,256]{0,1:T(8,128)(2,1)S(1)} %pad_maximum_fusion.1), channel_id=1, replica_groups=mesh['gx'=4,'gy'=4,'gz'=2] {'gz'}, dimensions={0}, use_global_device_ids=true | all-gather | bytes 786432 | tf_op jit(solution)/shard_map/all_gather | solution.py:46
  132.4 4.8 %while.43 = (s32[]{:T(128)}, f32[512]{0:T(512)S(1)}, f32[512]{0:T(512)S(1)}, s32[2]{0:T(128)S(1)}, s32[512]{0:T(512)S(1)}, /*index=5*/s32[2,8]{1,0:T(2,128)S(1)}...) while((s32[]{:T(128)}, f32[512]{0:T(512)S(1)}, ...), condition=%wide.region_7.8_spmd.clone, body=%wide.region_3.7_spmd.clone.sunk | while | flops 70803472 | bytes 2418638 | solution.py:84
  137.7 5.9 %while.44 = (s32[]{:T(128)}, f32[512,128]{1,0:T(8,128)S(1)}, s32[2]{0:T(128)S(1)}, s32[512]{0:T(512)S(1)}, s32[2,8]{1,0:T(2,128)S(1)}, /*index=5*/bf16[1024,256]...) while((s32[]{:T(128)}, f32[512,128]{1,0:T(8,128)S(1)}, ...), condition=%wide.region_10.11_spmd.clone, body=%wide.region_8.10_spmd.clone.sunk | while | flops 136467984 | bytes 945628 | solution.py:103
  139.1 1.5 fusion.118
  142.1 1.5 fusion.118
  143.8 47.6 %all-gather.16.cloned.1.call-done = bf16[512,4096]{1,0:T(8,128)(2,1)} async-done(((bf16[512,256]{1,0:T(8,128)(2,1)}), bf16[512,4096]{1,0:T(8,128)(2,1)}) %all-gather.16.cloned.1.call-update) | async-done | bytes 4194320 | tf_op jit(solution)/shard_map/all_gather | solution.py:116
  191.3 4.0 multiply_reduce_fusion
  196.0 9.3 %while.45 = (s32[]{:T(128)}, f32[512,128]{1,0:T(8,128)S(1)}, bf16[2,512,256]{1,2,0:T(8,128)(2,1)S(1)}, s32[2]{0:T(128)}, s32[512]{0:T(512)S(1)}, /*index=5*/s32[...) while((s32[]{:T(128)}, f32[512,128]{1,0:T(8,128)S(1)}, ...), condition=%wide.region_15.16_spmd.clone, body=%wide.region_13.15_spmd.clone.sunk | while | flops 339367424 | bytes 6974985 | solution.py:149
  206.4 3.9 convolution_convert_fusion.1
  211.1 8.2 %reduce-scatter.5.cloned.1.call-done = bf16[512,256]{1,0:T(8,128)(2,1)} async-done(((bf16[1024,256]{1,0:T(8,128)(2,1)}), bf16[512,256]{1,0:T(8,128)(2,1)}) %reduce-scatter.5.cloned.1.call-update) | async-done | bytes 262160 | tf_op jit(solution)/shard_map/reduce_scatter | solution.py:152
  220.2 5.8 %fusion.52 = bf16[4096,512]{0,1:T(8,128)(2,1)} fusion(bf16[3,4096,128]{1,2,0:T(8,128)(2,1)} %all-gather.10.cloned.1.call-done, bf16[1,512,128]{2,1,0:T(8,128)(2,1)S(1)} %get-tuple-element.713, bf16[1,512,128]{2,1,0:T(8,128)(2,1)S(1)} %get-tuple-element.712, bf16[1,512,128]{2,1,0:T(8,128)(2,1)S(1)} %convert_bitcast_fusion.1), kind=kOutput, calls=%fused_computation.84 | convolution fusion | flops 1613103104 | bytes 7733248 | tf_op jit(solution)/shard_map/mch,mth->ct/dot_general | solution.py:182
  226.3 6.1 %fusion.53 = bf16[3,4096,128]{1,2,0:T(8,128)(2,1)} fusion(bf16[512,4096]{1,0:T(8,128)(2,1)} %all-gather.8.cloned.1.call-done, bf16[1,512,128]{2,1,0:T(8,128)(2,1)S(1)} %get-tuple-element.713, bf16[1,512,128]{2,1,0:T(8,128)(2,1)S(1)} %get-tuple-element.712, bf16[1,512,128]{2,1,0:T(8,128)(2,1)S(1)} %convert_bitcast_fusion.1), kind=kOutput, calls=%fused_computation.85 | convolution fusion | flops 1612578816 | bytes 7733248 | tf_op jit(solution)/shard_map/tc,mth->mch/dot_general | solution.py:165
  232.4 1.3 copy.68
  233.8 5.5 %all-to-all-start = ((bf16[128,16,256]{2,0,1:T(8,128)(2,1)}), bf16[128,16,256]{2,0,1:T(8,128)(2,1)S(1)}, u32[]{:S(2)}, u32[]{:S(2)}) async-start(bf16[128,16,256]{2,0,1:T(8,128)(2,1)} %copy.68), calls=%async_computation | async-start | bytes 2097152 | tf_op jit(solution)/shard_map/all_to_all | solution.py:106
  239.3 3.1 reduce-scatter.11.cloned.1.call-done
  242.4 2.1 convert_element_type.104
  244.5 25.8 %all-to-all-done = bf16[128,16,256]{2,0,1:T(8,128)(2,1)S(1)} async-done(((bf16[128,16,256]{2,0,1:T(8,128)(2,1)}), bf16[128,16,256]{2,0,1:T(8,128)(2,1)S(1)}, u32[]{:S(2)}, u32[]{:S(2)}) %all-to-all-start) | async-done | bytes 1048608 | tf_op jit(solution)/shard_map/all_to_all | solution.py:106
  270.3 19.1 %all-gather.12.cloned.1.call-done = bf16[512,2048]{0,1:T(8,128)(2,1)} async-done(((bf16[512,128]{0,1:T(8,128)(2,1)}), bf16[512,2048]{0,1:T(8,128)(2,1)}) %all-gather.12.cloned.1.call-update) | async-done | bytes 2097168 | tf_op jit(solution)/shard_map/all_gather | solution.py:105
  289.4 4.8 %convolution_convert_fusion.2 = bf16[16,512,256]{2,1,0:T(8,128)(2,1)} fusion(bf16[512,16,128]{0,2,1:T(8,128)(2,1)} %bitcast.148, bf16[128,16,256]{2,0,1:T(8,128)(2,1)S(1)} %all-to-all-done), kind=kOutput, calls=%fused_computation.88 | convolution fusion | flops 538968064 | bytes 7340032 | tf_op jit(solution)/shard_map/thd,hdc->htc/dot_general | solution.py:108
  294.2 3.5 reduce_sum.108
  297.8 67.0 %reduce-scatter.7.cloned.1.call-done = bf16[256,512]{0,1:T(8,128)(2,1)} async-done(((bf16[4096,512]{0,1:T(8,128)(2,1)}), bf16[256,512]{0,1:T(8,128)(2,1)}) %reduce-scatter.7.cloned.1.call-update) | async-done | bytes 262160 | tf_op jit(solution)/shard_map/reduce_scatter | solution.py:181
  364.8 1.3 fusion.59
  366.1 30.5 %psum.14 = f32[512]{0:T(512)S(1)} all-reduce(f32[512]{0:T(512)S(1)} %fusion.59), channel_id=1, replica_groups=mesh['gx'=4,'gy'=4,'gz'=2] {'gx','gy'}, use_global_device_ids=true, to_apply=%region_19.20 | all-reduce | flops 512 | bytes 4096 | tf_op jit(solution)/shard_map/psum | solution.py:193
  396.6 1.5 fusion.63
  398.1 5.7 %psum.15 = f32[2,256]{1,0:T(2,128)} all-reduce(f32[2,256]{1,0:T(2,128)S(1)} %fusion.63), channel_id=1, replica_groups=mesh['gx'=4,'gy'=4,'gz'=2] {'gz'}, use_global_device_ids=true, to_apply=%region_22.23 | all-reduce | flops 512 | bytes 4096 | tf_op jit(solution)/shard_map/psum | solution.py:199
  403.8 6.4 %reduce-scatter.9.cloned.1.call-done = bf16[3,2048,128]{1,2,0:T(8,128)(2,1)} async-done(((bf16[3,4096,128]{1,2,0:T(8,128)(2,1)}), bf16[3,2048,128]{1,2,0:T(8,128)(2,1)}) %reduce-scatter.9.cloned.1.call-update) | async-done | bytes 1572880 | tf_op jit(solution)/shard_map/reduce_scatter | solution.py:172
  410.2 3.1 copy.76
  (146 shorter events, 21.5 us)
Async XLA Ops:
  7.2 2.8 copy-start
  7.2 37.1 %copy-start.12 = (s32[512]{0:T(512)S(1)}, s32[512]{0:T(512)}, u32[]{:S(2)}) copy-start(s32[512]{0:T(512)} %param.14) | copy-start | bytes 6148
  7.2 37.1 %copy-start.14 = (f32[2,256]{1,0:T(2,128)S(1)}, f32[2,256]{1,0:T(2,128)}, u32[]{:S(2)}) copy-start(f32[2,256]{1,0:T(2,128)} %param.16) | copy-start | bytes 6148
  7.2 38.2 %copy-start.4 = (bf16[128,2048]{1,0:T(8,128)(2,1)S(1)}, bf16[128,2048]{1,0:T(8,128)(2,1)}, u32[]{:S(2)}) copy-start(bf16[128,2048]{1,0:T(8,128)(2,1)} %param.18) | copy-start | bytes 1572868
  7.2 39.9 %copy-start.5 = (s32[2,8]{1,0:T(2,128)S(1)}, s32[2,8]{1,0:T(2,128)}, u32[]{:S(2)}) copy-start(s32[2,8]{1,0:T(2,128)} %param.15) | copy-start | bytes 196
  7.2 50.6 %all-gather.10.cloned.1.call-start = ((), (), s32[]{:S(2)}) async-start(), calls=%async_computation.6 | async-start | bytes 4718592 | tf_op jit(solution)/shard_map/all_gather | solution.py:35
  10.0 103.0 %all-gather.8.cloned.1.call-start = ((), (), s32[]{:S(2)}) async-start(), calls=%async_computation.5 | async-start | bytes 4456448 | tf_op jit(solution)/shard_map/all_gather | solution.py:40
  44.3 2.8 copy-start.10
  44.4 2.7 copy-start.8
  44.4 73.6 %copy-start.6 = (f32[1,256]{1,0:T(1,128)}, f32[1,256]{1,0:T(1,128)S(1)}, u32[]{:S(2)}) copy-start(f32[1,256]{1,0:T(1,128)S(1)} %get-tuple-element.714) | copy-start | bytes 3076
  45.3 98.4 %all-gather.14.cloned.1.call-start = ((), (), s32[]{:S(2)}) async-start(), calls=%async_computation.8 | async-start | bytes 1572864 | tf_op jit(solution)/shard_map/all_gather | solution.py:36
  46.4 144.9 %all-gather.16.cloned.1.call-start = ((), (), s32[]{:S(2)}) async-start(), calls=%async_computation.9 | async-start | bytes 4456448 | tf_op jit(solution)/shard_map/all_gather | solution.py:116
  47.0 172.3 %reduce-scatter.5.cloned.1.call-start = ((), (), s32[]{:S(2)}) async-start(), calls=%async_computation.10 | async-start | bytes 786432 | tf_op jit(solution)/shard_map/reduce_scatter | solution.py:152
  143.7 62.6 %copy-start.2 = (bf16[512,128]{0,1:T(8,128)(2,1)}, bf16[512,128]{0,1:T(8,128)(2,1)S(1)}, u32[]{:S(2)}) copy-start(bf16[512,128]{0,1:T(8,128)(2,1)S(1)} %copy.66) | copy-start | bytes 393220
  206.3 36.1 %reduce-scatter.11.cloned.1.call-start = ((), (), s32[]{:S(2)}) async-start(), calls=%async_computation.13 | async-start | bytes 1572864 | tf_op jit(solution)/shard_map/reduce_scatter | solution.py:175
  210.3 79.1 %all-gather.12.cloned.1.call-start = ((), (), s32[]{:S(2)}) async-start(), calls=%async_computation.7 | async-start | bytes 2228224 | tf_op jit(solution)/shard_map/all_gather | solution.py:105
  211.0 153.8 %reduce-scatter.7.cloned.1.call-start = ((), (), s32[]{:S(2)}) async-start(), calls=%async_computation.11 | async-start | bytes 4456448 | tf_op jit(solution)/shard_map/reduce_scatter | solution.py:181
  226.1 6.4 %copy-start.1 = (bf16[128,4096]{0,1:T(8,128)(2,1)S(1)}, bf16[128,4096]{0,1:T(8,128)(2,1)}, u32[]{:S(2)}) copy-start(bf16[128,4096]{0,1:T(8,128)(2,1)} %all-gather.14.cloned.1.call-done) | copy-start | bytes 3145732
  226.1 184.1 %reduce-scatter.9.cloned.1.call-start = ((), (), s32[]{:S(2)}) async-start(), calls=%async_computation.12 | async-start | bytes 4718592 | tf_op jit(solution)/shard_map/reduce_scatter | solution.py:172
  233.8 36.5 %all-to-all-start = ((bf16[128,16,256]{2,0,1:T(8,128)(2,1)}), bf16[128,16,256]{2,0,1:T(8,128)(2,1)S(1)}, u32[]{:S(2)}, u32[]{:S(2)}) async-start(bf16[128,16,256]{2,0,1:T(8,128)(2,1)} %copy.68), calls=%async_computation | async-start | bytes 2097152 | tf_op jit(solution)/shard_map/all_to_all | solution.py:106
  289.4 75.4 %copy-start.7 = (f32[1,256]{1,0:T(1,128)S(1)}, f32[1,256]{1,0:T(1,128)}, u32[]{:S(2)}) copy-start(f32[1,256]{1,0:T(1,128)} %copy-done.6) | copy-start | bytes 3076
  289.4 75.4 %copy-start.9 = (f32[1,256]{1,0:T(1,128)S(1)}, f32[1,256]{1,0:T(1,128)}, u32[]{:S(2)}) copy-start(f32[1,256]{1,0:T(1,128)} %copy-done.8) | copy-start | bytes 3076
  289.4 75.4 %copy-start.11 = (pred[512]{0:T(512)(128)(4,1)S(1)}, pred[512]{0:T(512)(128)(4,1)}, u32[]{:S(2)}) copy-start(pred[512]{0:T(512)(128)(4,1)} %copy-done.10) | copy-start | bytes 1540
  294.2 102.4 %copy-start.13 = (s32[512]{0:T(512)S(1)}, s32[512]{0:T(512)}, u32[]{:S(2)}) copy-start(s32[512]{0:T(512)} %param.14) | copy-start | bytes 6148
  364.8 48.5 %copy-start.3 = (bf16[256,512]{0,1:T(8,128)(2,1)S(1)}, bf16[256,512]{0,1:T(8,128)(2,1)}, u32[]{:S(2)}) copy-start(bf16[256,512]{0,1:T(8,128)(2,1)} %reduce-scatter.7.cloned.1.call-done) | copy-start | bytes 786436
Sparse Core Ops, SparseCore 0:
  10.1 47.6 all-gather.9
  60.5 52.4 all-gather.7
  115.1 23.5 all-gather.13
  140.6 50.6 all-gather.15
  206.4 12.7 reduce-scatter.4
  221.9 20.3 reduce-scatter.10
  245.1 44.2 all-gather.11
  293.3 71.4 reduce-scatter.6
  367.6 42.5 reduce-scatter.8
